TPU v7x, 512 devices: a whole 4x8x8 slice. The times are simulated.
512 devices in a mesh: blk: 128 (over z_lo, y, x), freq: 4 (over z_hi, core).
Axes of the slice: x: 4, y: 8, z: 8 (z_hi: 2, z_lo: 4; z = z_hi * 4 + z_lo), core: 2. Of those that a mesh axis runs over, the one named last changes fastest.
Arguments:
- node_index: int32 [3, 16384], P(None, 'blk'), may hold values from 0 to 63
- emitters: int32 [64], replicated, may hold values from 0 to 16383
- admittance: float32 [2, 16384], P(None, 'blk'), may hold values from -3 to 3
- wavenumbers: float32 [4], P('freq'), may hold values from 20 to 60
Outputs:
- scattered: bfloat16 [4, 2, 64, 16384], P('freq', None, None, 'blk')
- gradient: float32 [16384], P('blk')
All inputs are finite; a program needn't handle non-finite values.
Results may differ from a plain program's by a relative error of at most 0.006.
Values may be sent and summed in bfloat16 or wider, within the bound.
No kernel may reach another device: no remote copies, remote signals or barrier semaphores. Data moves between devices by JAX's collectives and lax.ppermute only.
A program may use at most 64 MiB of HBM per device.

v0:
```python
import jax
import jax.numpy as jnp
from jax import lax
from jax.sharding import Mesh
from jax.sharding import PartitionSpec as P

GRID = 64
BLK = ("blk_0", "blk_1", "blk_2")
soften = 0.0025


def in_order(blocks, dim):
    blocks = jnp.moveaxis(blocks, 0, dim)
    shape = blocks.shape
    return blocks.reshape(*shape[:dim], shape[dim] * shape[dim + 1], *shape[dim + 2 :])


def all_blocks(value, axes, turns):
    blocks = value
    for k in turns:
        blocks = lax.all_gather(blocks, axes[k])
    done = turns[::-1]
    back = [done.index(k) for k in range(len(axes))]
    blocks = blocks.transpose(*back, *range(len(axes), blocks.ndim))
    return blocks.reshape(-1, *value.shape)


def gather_axes(value, axes, turns, dim):
    return in_order(all_blocks(value, axes, turns), dim)


def copy_for_each(value, axis):
    copies = jnp.broadcast_to(value, (lax.axis_size(axis), *value.shape))
    return lax.all_to_all(copies, axis, split_axis=0, concat_axis=0, tiled=True)


def taken_together(value, axis):
    return copy_for_each(value, axis).sum(axis=0)


def green_tile(row_places, col_places, wavenum, strength):
    separation = row_places[:, :, None] - col_places[:, None, :]
    radius = jnp.sqrt(jnp.sum(separation * separation, axis=0) + soften)
    amplitude = strength / radius
    phase_turn = wavenum * radius
    return jnp.stack([amplitude * jnp.cos(phase_turn), amplitude * jnp.sin(phase_turn)]).astype(
        jnp.bfloat16
    )


def apply_tile(tile_data, source):
    real_part = jnp.einsum(
        "tc,rc->tr", source[0], tile_data[0], preferred_element_type=jnp.float32
    ) - jnp.einsum("tc,rc->tr", source[1], tile_data[1], preferred_element_type=jnp.float32)
    imag_part = jnp.einsum(
        "tc,rc->tr", source[1], tile_data[0], preferred_element_type=jnp.float32
    ) + jnp.einsum("tc,rc->tr", source[0], tile_data[1], preferred_element_type=jnp.float32)
    return jnp.stack([real_part, imag_part])


def complex_scale(factor_pair, field_pair):
    factor_real = factor_pair[0][None, :]
    factor_imag = factor_pair[1][None, :]
    real_part = factor_real * field_pair[0] - factor_imag * field_pair[1]
    imag_part = factor_real * field_pair[1] + factor_imag * field_pair[0]
    return jnp.stack([real_part, imag_part])


def row_potential(places, own_places, wavenum, strength, block_count, row_count):
    group_blocks = 1
    for candidate in range(1, block_count + 1):
        if block_count % candidate == 0 and candidate * row_count <= 4096:
            group_blocks = candidate
    group_cols = group_blocks * row_count

    def make_tile(group_id):
        col_places = lax.dynamic_slice_in_dim(places, group_id * group_cols, group_cols, 1)
        return green_tile(own_places, col_places, wavenum, strength)

    tile_stack = lax.map(make_tile, jnp.arange(block_count // group_blocks, dtype=jnp.int32))
    tile_flat = jnp.transpose(tile_stack, (1, 2, 0, 3)).reshape(
        2, row_count, block_count * row_count
    )

    def potential(source, whole_source):
        if whole_source is None:
            whole_source = gather_axes(source, BLK, (0, 1, 2), 2)
        return apply_tile(tile_flat, whole_source)

    return potential


def local(node_index, emitters, admittance, wavenumbers):
    block_count = lax.axis_size(BLK)
    lane_count = lax.axis_size("freq")
    row_count = node_index.shape[1]
    node_count = block_count * row_count
    emitter_count = emitters.shape[0]
    own_block = lax.axis_index(BLK)
    every_index = lax.all_gather(node_index, BLK, axis=1, tiled=True)
    places = every_index.astype(jnp.float32) / GRID
    own_places = node_index.astype(jnp.float32) / GRID
    wavenum = wavenumbers[0]
    strength = float(node_count) ** (-0.5)
    emitter_places = places[:, emitters]
    incident_whole = green_tile(emitter_places, places, wavenum, 1.0)
    incident = lax.dynamic_slice_in_dim(incident_whole, own_block * row_count, row_count, 2)
    potential = row_potential(places, own_places, wavenum, strength, block_count, row_count)
    first_wave = potential(incident, incident_whole)
    weighted = complex_scale(admittance, first_wave).astype(jnp.bfloat16)
    second = potential(weighted, None)
    lane_terms = jnp.sum(first_wave[0] * second[0] - first_wave[1] * second[1], axis=0) / (
        lane_count * emitter_count
    )
    gradient = taken_together(lane_terms, "freq")
    return (second.astype(jnp.bfloat16)[None], gradient)


def solution(mesh):
    split = Mesh(
        mesh.devices.reshape(4, 8, 4, mesh.shape["freq"]), ("blk_0", "blk_1", "blk_2", "freq")
    )
    in_specs = (P(None, BLK), P(), P(None, BLK), P("freq"))
    out_specs = (P("freq", None, None, BLK), P(BLK))
    return jax.shard_map(local, mesh=split, in_specs=in_specs, out_specs=out_specs, check_vma=False)
```

profile of v0, /device:TPU:1, one launch (start us, length us, event | category | flops | bytes accessed | tf_op | source)
XLA Modules:
  0.0 678.0 jit_solution(9046614232390934011)
XLA Ops:
  8.7 366.5 %all_gather.19 = s32[3,16384]{0,1:T(8,128)S(1)} all-gather(s32[3,128]{0,1:T(8,128)S(1)} %copy.41), channel_id=1, replica_groups=mesh['blk_0'=4,'blk_1'=8,'blk_2'=4,'freq'=4] {'blk_0','blk_1','blk_2'}, dimensions={1}, use_global_device_ids=true | all-gather | bytes 198144 | tf_op jit(solution)/shard_map/all_gather | solution.py:100
  375.2 3.5 convert_multiply_fusion
  378.8 5.5 copy.43
  384.3 4.0 gather_fusion
  389.0 3.6 multiply_reduce_fusion.1
  392.5 68.6 %while.10 = (s32[]{:T(128)}, bf16[4,2,128,4096]{2,3,0,1:T(8,128)(2,1)}, f32[3,128]{1,0:T(4,128)S(1)}, s32[4]{0:T(128)S(1)}, f32[3,16384]{1,0:T(4,128)S(1)}, /*in...) while((s32[]{:T(128)}, bf16[4,2,128,4096]{2,3,0,1:T(8,128)(2,1)}, f32[3,128]{1,0:T(4,128)S(1)}, ...), condition=%wide.region_3.4_spmd, body=%wide.region_1.3_spmd.sunk | while | flops 8912902 | bytes 19023540 | solution.py:80
  394.6 8.9 %fusion.43 = (bf16[1,1,128,4096]{3,2,1,0:T(8,128)(2,1)S(1)}, bf16[1,1,128,4096]{3,2,1,0:T(8,128)(2,1)S(1)}) fusion(f32[]{:T(128)} %get-tuple-element.164, f32[128,4096]{1,0:T(8,128)S(1)} %multiply_reduce_fusion.3), kind=kLoop, calls=%fused_computation.7.clone.1 | loop fusion | flops 3670016 | bytes 4194308 | tf_op jit(solution)/shard_map/while/body/eval_jaxpr/stack | solution.py:46
  403.6 1.5 pad_maximum_fusion.4
  405.1 3.1 copy.77
  411.8 8.9 %fusion.43 = (bf16[1,1,128,4096]{3,2,1,0:T(8,128)(2,1)S(1)}, bf16[1,1,128,4096]{3,2,1,0:T(8,128)(2,1)S(1)}) fusion(f32[]{:T(128)} %get-tuple-element.164, f32[128,4096]{1,0:T(8,128)S(1)} %multiply_reduce_fusion.3), kind=kLoop, calls=%fused_computation.7.clone.1 | loop fusion | flops 3670016 | bytes 4194308 | tf_op jit(solution)/shard_map/while/body/eval_jaxpr/stack | solution.py:46
  420.7 1.5 pad_maximum_fusion.4
  422.2 3.1 copy.77
  425.4 1.5 constant_dynamic-update-slice_fusion.2
  428.9 8.9 %fusion.43 = (bf16[1,1,128,4096]{3,2,1,0:T(8,128)(2,1)S(1)}, bf16[1,1,128,4096]{3,2,1,0:T(8,128)(2,1)S(1)}) fusion(f32[]{:T(128)} %get-tuple-element.164, f32[128,4096]{1,0:T(8,128)S(1)} %multiply_reduce_fusion.3), kind=kLoop, calls=%fused_computation.7.clone.1 | loop fusion | flops 3670016 | bytes 4194308 | tf_op jit(solution)/shard_map/while/body/eval_jaxpr/stack | solution.py:46
  437.9 1.5 pad_maximum_fusion.4
  439.4 3.1 copy.77
  446.1 8.9 %fusion.43 = (bf16[1,1,128,4096]{3,2,1,0:T(8,128)(2,1)S(1)}, bf16[1,1,128,4096]{3,2,1,0:T(8,128)(2,1)S(1)}) fusion(f32[]{:T(128)} %get-tuple-element.164, f32[128,4096]{1,0:T(8,128)S(1)} %multiply_reduce_fusion.3), kind=kLoop, calls=%fused_computation.7.clone.1 | loop fusion | flops 3670016 | bytes 4194308 | tf_op jit(solution)/shard_map/while/body/eval_jaxpr/stack | solution.py:46
  455.0 1.5 pad_maximum_fusion.4
  456.6 3.1 copy.77
  459.7 1.5 constant_dynamic-update-slice_fusion.2
  461.2 3.9 fusion.24
  465.8 16.6 %multiply_convert_fusion.2 = (bf16[64,16384]{1,0:T(8,128)(2,1)S(1)}, bf16[64,16384]{1,0:T(8,128)(2,1)S(1)}) fusion(f32[64,16384]{1,0:T(8,128)S(1)} %copy-done.4, f32[]{:T(128)} %bitcast.66), kind=kLoop, calls=%fused_computation.13 | loop fusion | flops 7340032 | bytes 8388612 | tf_op jit(solution)/shard_map/slice | solution.py:54
  486.0 11.2 %all_gather.20 = bf16[4,2,64,128]{3,2,1,0:T(8,128)(2,1)} all-gather(bf16[1,2,64,128]{3,2,1,0:T(8,128)(2,1)S(1)} %pad_maximum_fusion.1), channel_id=1, replica_groups=mesh['blk_0'=4,'blk_1'=8,'blk_2'=4,'freq'=4] {'blk_0'}, dimensions={0}, use_global_device_ids=true | all-gather | bytes 163840 | tf_op jit(solution)/shard_map/all_gather | solution.py:21
  497.4 84.1 %all-gather.5.cloned.1.call-done = bf16[32,2,64,128]{3,2,1,0:T(8,128)(2,1)} async-done(((bf16[4,2,64,128]{3,2,1,0:T(8,128)(2,1)}), bf16[32,2,64,128]{3,2,1,0:T(8,128)(2,1)}) %all-gather.5.cloned.1.call-update) | async-done | bytes 1048592 | tf_op jit(solution)/shard_map/all_gather | solution.py:21
  581.6 59.3 %all-gather.7.cloned.1.call-done = bf16[32,4,2,64,128]{4,3,2,1,0:T(8,128)(2,1)} async-done(((bf16[8,4,2,64,128]{4,3,2,1,0:T(8,128)(2,1)}), bf16[32,4,2,64,128]{4,3,2,1,0:T(8,128)(2,1)}) %all-gather.7.cloned.1.call-update) | async-done | bytes 4194320 | tf_op jit(solution)/shard_map/all_gather | solution.py:21
  640.8 3.1 copy.46
  647.2 1.6 fusion.6
  648.8 1.6 fusion.4
  651.7 1.6 fusion.16
  653.3 1.5 subtract_reduce_fusion
  655.5 8.2 %all-to-all-start = ((f32[4,1,128]{2,1,0:T(1,128)}), f32[4,1,128]{2,1,0:T(1,128)S(1)}, u32[]{:S(2)}, u32[]{:S(2)}) async-start(f32[4,1,128]{2,1,0:T(1,128)} %broadcast_in_dim.18), calls=%async_computation | async-start | bytes 4096 | tf_op jit(solution)/shard_map/all_to_all | solution.py:34
  664.3 6.4 all-to-all-done
  (53 shorter events, 21.1 us)
Async XLA Ops:
  7.2 574.4 %all-gather.5.cloned.1.call-start = ((), (), s32[]{:S(2)}) async-start(), calls=%async_computation.1 | async-start | bytes 1179648 | tf_op jit(solution)/shard_map/all_gather | solution.py:21
  378.8 5.5 copy-start.6
  461.2 4.7 copy-start.4
  465.1 18.2 %copy-start.2 = (bf16[1,128,4,4096]{1,3,2,0:T(8,128)(2,1)}, bf16[1,128,4,4096]{1,3,2,0:T(8,128)(2,1)S(1)}, u32[]{:S(2)}) copy-start(bf16[1,128,4,4096]{1,3,2,0:T(8,128)(2,1)S(1)} %get-tuple-element.86) | copy-start | bytes 12582916
  465.1 20.0 %copy-start = (bf16[1,128,4,4096]{1,3,2,0:T(8,128)(2,1)}, bf16[1,128,4,4096]{1,3,2,0:T(8,128)(2,1)S(1)}, u32[]{:S(2)}) copy-start(bf16[1,128,4,4096]{1,3,2,0:T(8,128)(2,1)S(1)} %get-tuple-element.85) | copy-start | bytes 12582916
  485.1 0.9 copy-start.5
  497.2 143.6 %all-gather.7.cloned.1.call-start = ((), (), s32[]{:S(2)}) async-start(), calls=%async_computation.2 | async-start | bytes 5242880 | tf_op jit(solution)/shard_map/all_gather | solution.py:21
  645.0 2.2 copy-start.1
  646.3 2.4 copy-start.3
  655.5 15.2 %all-to-all-start = ((f32[4,1,128]{2,1,0:T(1,128)}), f32[4,1,128]{2,1,0:T(1,128)S(1)}, u32[]{:S(2)}, u32[]{:S(2)}) async-start(f32[4,1,128]{2,1,0:T(1,128)} %broadcast_in_dim.18), calls=%async_computation | async-start | bytes 4096 | tf_op jit(solution)/shard_map/all_to_all | solution.py:34
Sparse Core Ops, SparseCore 0:
  497.3 84.1 all-gather.4
  583.6 57.1 all-gather.6
where the time goes:
time: 679 us; the launch traced here: 678 us
  blocking collectives  378 us (56%)
  waiting for transfers between devices  150 us (22%)
  other arithmetic  70.8 us (10%)
  local copies, waits for them, and re-layouts  43.9 us (6%)
  between operations  14.9 us (2%)
  matrix products  9.75 us (1%)
  starting transfers between devices  8.47 us (1%)
    all_gather x1, blocking collectives, local(): every_index = lax.all_gather(node_index, BLK, axis=1, tiled=True)  367 us
    all_gather x2, waiting for transfers between devices, all_blocks(): blocks = lax.all_gather(blocks, axes[k])  143 us
    another operation x8, other arithmetic, green_tile(): jnp.stack([amplitude * jnp.cos(phase_turn), amplitude * jnp.sin(phase_tur...  41.8 us
    dynamic_update_slice x8, local copies, waits for them, and re-layouts, row_potential(): lax.map(make_tile, jnp.arange(block_count // group_blocks, dtype=jnp.int32))  18.3 us
    slice x1, other arithmetic, apply_tile(): source[1]  16.6 us
  transfers between devices with their start and end apart: 3, of which 3 were waited for; matrix products, arithmetic and copies ran while one was open for 0% of the time, Pallas kernels for 0%

commit v1 on v0

--- a/solution.py
+++ b/solution.py
@@ -97,7 +97,9 @@
     node_count = block_count * row_count
     emitter_count = emitters.shape[0]
     own_block = lax.axis_index(BLK)
-    every_index = lax.all_gather(node_index, BLK, axis=1, tiled=True)
+    every_index = jnp.concatenate(
+        lax.all_to_all(jnp.stack([node_index] * lax.axis_size(BLK)), BLK, 0, 0), axis=1
+    )
     places = every_index.astype(jnp.float32) / GRID
     own_places = node_index.astype(jnp.float32) / GRID
     wavenum = wavenumbers[0]

time: 679 us -> 296 us (0.44)
  blocking collectives: 378 us -> 11.6 us
  waiting for transfers between devices: 150 us -> 112 us
  starting transfers between devices: 8.47 us -> 26.2 us
    all_gather x1 -> x0, blocking collectives: 367 us -> none  [local(): every_index = lax.all_gather(node_index, BLK, axis=1, tiled=True)]
    all_gather x2, waiting for transfers between devices: 143 us -> 95.7 us  [all_blocks(): blocks = lax.all_gather(blocks, axes[k])]
    all_to_all x0 -> x1, starting transfers between devices: none -> 17.8 us  [local(): lax.all_to_all(jnp.stack([node_index] * lax.axis_size(BLK)), BLK, 0, 0)]
    all_to_all x0 -> x1, waiting for transfers between devices: none -> 10.2 us  [local(): lax.all_to_all(jnp.stack([node_index] * lax.axis_size(BLK)), BLK, 0, 0)]
  transfers between devices with their start and end apart: 3 -> 4, of which waited for: 3 -> 4; matrix products, arithmetic and copies ran while one was open for 0% -> 1% of each run, Pallas kernels for 0% -> 0%
where the time goes in v1:
time: 296 us
  waiting for transfers between devices  112 us (38%)
  other arithmetic  68 us (23%)
  local copies, waits for them, and re-layouts  50.2 us (17%)
  starting transfers between devices  26.2 us (9%)
  between operations  14.9 us (5%)
  blocking collectives  11.6 us (4%)
  matrix products  9.74 us (3%)
    all_gather x2, waiting for transfers between devices, all_blocks(): blocks = lax.all_gather(blocks, axes[k])  95.7 us
    another operation x8, other arithmetic, green_tile(): jnp.stack([amplitude * jnp.cos(phase_turn), amplitude * jnp.sin(phase_tur...  41.8 us
    dynamic_update_slice x8, local copies, waits for them, and re-layouts, row_potential(): lax.map(make_tile, jnp.arange(block_count // group_blocks, dtype=jnp.int32))  18.3 us
    all_to_all x1, starting transfers between devices, local(): lax.all_to_all(jnp.stack([node_index] * lax.axis_size(BLK)), BLK, 0, 0)  17.8 us
    slice x1, other arithmetic, apply_tile(): source[1]  16.6 us
    all_gather x1, blocking collectives, all_blocks(): blocks = lax.all_gather(blocks, axes[k])  11.6 us
    div x2, local copies, waits for them, and re-layouts, local(): places = every_index.astype(jnp.float32) / GRID  10.3 us
    all_to_all x1, waiting for transfers between devices, local(): lax.all_to_all(jnp.stack([node_index] * lax.axis_size(BLK)), BLK, 0, 0)  10.2 us
  transfers between devices with their start and end apart: 4, of which 4 were waited for; matrix products, arithmetic and copies ran while one was open for 1% of the time, Pallas kernels for 0%

profile of v1, /device:TPU:1, one launch (start us, length us, event | category | flops | bytes accessed | tf_op | source)
XLA Modules:
  0.0 295.6 jit_solution(10298264470148744374)
XLA Ops:
  8.6 17.8 %all-to-all-start = ((s32[128,3,128]{2,1,0:T(4,128)}), s32[128,3,128]{2,1,0:T(4,128)S(1)}, u32[]{:S(2)}, u32[]{:S(2)}) async-start(s32[128,3,128]{2,1,0:T(4,128)} %stack.21), calls=%async_computation | async-start | bytes 524288 | tf_op jit(solution)/shard_map/all_to_all | solution.py:101
  29.2 10.2 %all-to-all-done = s32[128,3,128]{2,1,0:T(4,128)S(1)} async-done(((s32[128,3,128]{2,1,0:T(4,128)}), s32[128,3,128]{2,1,0:T(4,128)S(1)}, u32[]{:S(2)}, u32[]{:S(2)}) %all-to-all-start) | async-done | bytes 196640 | tf_op jit(solution)/shard_map/all_to_all | solution.py:101
  39.5 4.9 %copy.41 = f32[3,128,128]{0,2,1:T(8,128)} copy(f32[3,128,128]{2,0,1:T(4,128)S(1)} %multiply_bitcast_fusion) | data formatting | bytes 393216 | tf_op jit(solution)/shard_map/div | solution.py:103
  44.4 5.4 %copy.43 = f32[3,16384]{1,0:T(4,128)S(1)} copy(f32[3,16384]{0,1:T(8,128)} %bitcast.78) | data formatting | bytes 393216 | tf_op jit(solution)/shard_map/div | solution.py:103
  49.8 4.0 %gather_fusion = f32[64,3]{1,0:T(8,128)S(1)} fusion(f32[3,16384]{0,1:T(8,128)} %bitcast.79, s32[1024]{0:T(1024)S(1)} %pad_clamp_fusion), kind=kCustom, calls=%fused_computation | custom fusion | bytes 1792 | tf_op jit(solution)/shard_map/gather | solution.py:107
  53.9 3.6 %multiply_reduce_fusion.1 = f32[64,16384]{1,0:T(8,128)} fusion(f32[3,16384]{1,0:T(4,128)S(1)} %copy.43, f32[3,64]{1,0:T(4,128)S(1)} %copy.42), kind=kLoop, calls=%fused_computation.11 | loop fusion | flops 8388608 | bytes 4391680 | tf_op jit(solution)/shard_map/reduce_sum | solution.py:43
  57.5 68.6 %while.10 = (s32[]{:T(128)}, bf16[4,2,128,4096]{2,3,0,1:T(8,128)(2,1)}, f32[3,128]{1,0:T(4,128)S(1)}, s32[4]{0:T(128)S(1)}, f32[3,16384]{1,0:T(4,128)S(1)}, /*in...) while((s32[]{:T(128)}, bf16[4,2,128,4096]{2,3,0,1:T(8,128)(2,1)}, f32[3,128]{1,0:T(4,128)S(1)}, ...), condition=%wide.region_3.4_spmd, body=%wide.region_1.3_spmd.sunk | while | flops 8912902 | bytes 19023540 | solution.py:80
  59.6 8.9 %fusion.43 = (bf16[1,1,128,4096]{3,2,1,0:T(8,128)(2,1)S(1)}, bf16[1,1,128,4096]{3,2,1,0:T(8,128)(2,1)S(1)}) fusion(f32[]{:T(128)} %get-tuple-element.164, f32[128,4096]{1,0:T(8,128)S(1)} %multiply_reduce_fusion.3), kind=kLoop, calls=%fused_computation.7.clone.1 | loop fusion | flops 3670016 | bytes 4194308 | tf_op jit(solution)/shard_map/while/body/eval_jaxpr/stack | solution.py:46
  68.5 1.5 pad_maximum_fusion.4
  70.0 3.1 %copy.77 = bf16[1,2,128,4096]{2,3,0,1:T(8,128)(2,1)S(1)} copy(bf16[1,2,128,4096]{3,2,1,0:T(8,128)(2,1)} %pad_maximum_fusion.4) | data formatting | bytes 4194304 | tf_op jit(solution)/shard_map/while/body/jit(dynamic_update_index_in_dim)/dynamic_update_slice | solution.py:80
  76.7 8.9 %fusion.43 = (bf16[1,1,128,4096]{3,2,1,0:T(8,128)(2,1)S(1)}, bf16[1,1,128,4096]{3,2,1,0:T(8,128)(2,1)S(1)}) fusion(f32[]{:T(128)} %get-tuple-element.164, f32[128,4096]{1,0:T(8,128)S(1)} %multiply_reduce_fusion.3), kind=kLoop, calls=%fused_computation.7.clone.1 | loop fusion | flops 3670016 | bytes 4194308 | tf_op jit(solution)/shard_map/while/body/eval_jaxpr/stack | solution.py:46
  85.7 1.5 pad_maximum_fusion.4
  87.2 3.1 %copy.77 = bf16[1,2,128,4096]{2,3,0,1:T(8,128)(2,1)S(1)} copy(bf16[1,2,128,4096]{3,2,1,0:T(8,128)(2,1)} %pad_maximum_fusion.4) | data formatting | bytes 4194304 | tf_op jit(solution)/shard_map/while/body/jit(dynamic_update_index_in_dim)/dynamic_update_slice | solution.py:80
  93.9 8.9 %fusion.43 = (bf16[1,1,128,4096]{3,2,1,0:T(8,128)(2,1)S(1)}, bf16[1,1,128,4096]{3,2,1,0:T(8,128)(2,1)S(1)}) fusion(f32[]{:T(128)} %get-tuple-element.164, f32[128,4096]{1,0:T(8,128)S(1)} %multiply_reduce_fusion.3), kind=kLoop, calls=%fused_computation.7.clone.1 | loop fusion | flops 3670016 | bytes 4194308 | tf_op jit(solution)/shard_map/while/body/eval_jaxpr/stack | solution.py:46
  102.8 1.5 pad_maximum_fusion.4
  104.3 3.1 %copy.77 = bf16[1,2,128,4096]{2,3,0,1:T(8,128)(2,1)S(1)} copy(bf16[1,2,128,4096]{3,2,1,0:T(8,128)(2,1)} %pad_maximum_fusion.4) | data formatting | bytes 4194304 | tf_op jit(solution)/shard_map/while/body/jit(dynamic_update_index_in_dim)/dynamic_update_slice | solution.py:80
  111.0 8.9 %fusion.43 = (bf16[1,1,128,4096]{3,2,1,0:T(8,128)(2,1)S(1)}, bf16[1,1,128,4096]{3,2,1,0:T(8,128)(2,1)S(1)}) fusion(f32[]{:T(128)} %get-tuple-element.164, f32[128,4096]{1,0:T(8,128)S(1)} %multiply_reduce_fusion.3), kind=kLoop, calls=%fused_computation.7.clone.1 | loop fusion | flops 3670016 | bytes 4194308 | tf_op jit(solution)/shard_map/while/body/eval_jaxpr/stack | solution.py:46
  120.0 1.5 pad_maximum_fusion.4
  121.5 3.1 %copy.77 = bf16[1,2,128,4096]{2,3,0,1:T(8,128)(2,1)S(1)} copy(bf16[1,2,128,4096]{3,2,1,0:T(8,128)(2,1)} %pad_maximum_fusion.4) | data formatting | bytes 4194304 | tf_op jit(solution)/shard_map/while/body/jit(dynamic_update_index_in_dim)/dynamic_update_slice | solution.py:80
  124.6 1.5 constant_dynamic-update-slice_fusion.2
  126.1 3.9 %fusion.24 = (bf16[1,128,4,4096]{1,3,2,0:T(8,128)(2,1)S(1)}, bf16[1,128,4,4096]{1,3,2,0:T(8,128)(2,1)S(1)}) fusion(bf16[2,128,4,4096]{1,3,2,0:T(8,128)(2,1)} %bitcast.85), kind=kLoop, calls=%fused_computation.48 | loop fusion | bytes 16777216 | tf_op jit(solution)/shard_map/slice | solution.py:54
  130.7 16.6 %multiply_convert_fusion.2 = (bf16[64,16384]{1,0:T(8,128)(2,1)S(1)}, bf16[64,16384]{1,0:T(8,128)(2,1)S(1)}) fusion(f32[64,16384]{1,0:T(8,128)S(1)} %copy-done.4, f32[]{:T(128)} %bitcast.69), kind=kLoop, calls=%fused_computation.12 | loop fusion | flops 7340032 | bytes 8388612 | tf_op jit(solution)/shard_map/slice | solution.py:54
  150.9 11.6 %all_gather.16 = bf16[4,2,64,128]{3,2,1,0:T(8,128)(2,1)} all-gather(bf16[1,2,64,128]{3,2,1,0:T(8,128)(2,1)S(1)} %pad_maximum_fusion.1), channel_id=1, replica_groups=mesh['blk_0'=4,'blk_1'=8,'blk_2'=4,'freq'=4] {'blk_0'}, dimensions={0}, use_global_device_ids=true | all-gather | bytes 163840 | tf_op jit(solution)/shard_map/all_gather | solution.py:21
  162.7 36.4 %all-gather.5.cloned.1.call-done = bf16[32,2,64,128]{3,2,1,0:T(8,128)(2,1)} async-done(((bf16[4,2,64,128]{3,2,1,0:T(8,128)(2,1)}), bf16[32,2,64,128]{3,2,1,0:T(8,128)(2,1)}) %all-gather.5.cloned.1.call-update) | async-done | bytes 1048592 | tf_op jit(solution)/shard_map/all_gather | solution.py:21
  199.2 59.3 %all-gather.7.cloned.1.call-done = bf16[32,4,2,64,128]{4,3,2,1,0:T(8,128)(2,1)} async-done(((bf16[8,4,2,64,128]{4,3,2,1,0:T(8,128)(2,1)}), bf16[32,4,2,64,128]{4,3,2,1,0:T(8,128)(2,1)}) %all-gather.7.cloned.1.call-update) | async-done | bytes 4194320 | tf_op jit(solution)/shard_map/all_gather | solution.py:21
  258.4 3.1 %copy.46 = bf16[4,8,4,2,64,128]{5,4,3,2,1,0:T(8,128)(2,1)S(1)} copy(bf16[4,8,4,2,64,128]{5,4,3,0,1,2:T(8,128)(2,1)} %bitcast.86) | data formatting | bytes 8388608 | tf_op jit(solution)/shard_map/transpose | solution.py:24
  264.8 1.6 fusion.6
  266.4 1.6 fusion.4
  269.3 1.6 fusion.16
  270.9 1.5 subtract_reduce_fusion
  273.1 8.2 %all-to-all-start.1 = ((f32[4,1,128]{2,1,0:T(1,128)}), f32[4,1,128]{2,1,0:T(1,128)S(1)}, u32[]{:S(2)}, u32[]{:S(2)}) async-start(f32[4,1,128]{2,1,0:T(1,128)} %broadcast_in_dim.18), calls=%async_computation.1 | async-start | bytes 4096 | tf_op jit(solution)/shard_map/all_to_all | solution.py:34
  281.9 6.4 %all-to-all-done.1 = f32[4,1,128]{2,1,0:T(1,128)S(1)} async-done(((f32[4,1,128]{2,1,0:T(1,128)}), f32[4,1,128]{2,1,0:T(1,128)S(1)}, u32[]{:S(2)}, u32[]{:S(2)}) %all-to-all-start.1) | async-done | bytes 2080 | tf_op jit(solution)/shard_map/all_to_all | solution.py:34
  (51 shorter events, 24.6 us)
Async XLA Ops:
  8.6 30.8 %all-to-all-start = ((s32[128,3,128]{2,1,0:T(4,128)}), s32[128,3,128]{2,1,0:T(4,128)S(1)}, u32[]{:S(2)}, u32[]{:S(2)}) async-start(s32[128,3,128]{2,1,0:T(4,128)} %stack.21), calls=%async_computation | async-start | bytes 524288 | tf_op jit(solution)/shard_map/all_to_all | solution.py:101
  26.4 172.8 %all-gather.5.cloned.1.call-start = ((), (), s32[]{:S(2)}) async-start(), calls=%async_computation.2 | async-start | bytes 1179648 | tf_op jit(solution)/shard_map/all_gather | solution.py:21
  126.1 4.7 %copy-start.4 = (f32[64,16384]{1,0:T(8,128)S(1)}, f32[64,16384]{1,0:T(8,128)}, u32[]{:S(2)}) copy-start(f32[64,16384]{1,0:T(8,128)} %multiply_reduce_fusion.1) | copy-start | bytes 12582916
  130.0 18.2 %copy-start.2 = (bf16[1,128,4,4096]{1,3,2,0:T(8,128)(2,1)}, bf16[1,128,4,4096]{1,3,2,0:T(8,128)(2,1)S(1)}, u32[]{:S(2)}) copy-start(bf16[1,128,4,4096]{1,3,2,0:T(8,128)(2,1)S(1)} %get-tuple-element.86) | copy-start | bytes 12582916
  130.0 20.0 %copy-start = (bf16[1,128,4,4096]{1,3,2,0:T(8,128)(2,1)}, bf16[1,128,4,4096]{1,3,2,0:T(8,128)(2,1)S(1)}, u32[]{:S(2)}) copy-start(bf16[1,128,4,4096]{1,3,2,0:T(8,128)(2,1)S(1)} %get-tuple-element.85) | copy-start | bytes 12582916
  162.5 95.9 %all-gather.7.cloned.1.call-start = ((), (), s32[]{:S(2)}) async-start(), calls=%async_computation.3 | async-start | bytes 5242880 | tf_op jit(solution)/shard_map/all_gather | solution.py:21
  262.6 2.2 copy-start.1
  263.9 2.4 copy-start.3
  273.1 15.2 %all-to-all-start.1 = ((f32[4,1,128]{2,1,0:T(1,128)}), f32[4,1,128]{2,1,0:T(1,128)S(1)}, u32[]{:S(2)}, u32[]{:S(2)}) async-start(f32[4,1,128]{2,1,0:T(1,128)} %broadcast_in_dim.18), calls=%async_computation.1 | async-start | bytes 4096 | tf_op jit(solution)/shard_map/all_to_all | solution.py:34
Sparse Core Ops, SparseCore 0:
  162.6 36.4 all-gather.4
  201.2 57.1 all-gather.6
